TPU v7x, 32 devices: a whole 2x2x4 slice. The times are simulated.
32 devices in a mesh: batch: 4 (over y, x), seq: 4 (over z), head: 2 (over core).
Axes of the slice: x: 2, y: 2, z: 4, core: 2. Of those that a mesh axis runs over, the one named last changes fastest.
Arguments:
- queries: bfloat16 [1, 6144, 2048], P(None, ('batch', 'seq'), 'head'), parts along dimension 1, may hold values from -240 to 240
- keys: bfloat16 [1, 6144, 1024], P(None, ('batch', 'seq'), 'head'), parts along dimension 1, may hold values from -6 to 6
- values: bfloat16 [1, 6144, 1024], P(None, ('batch', 'seq'), 'head'), parts along dimension 1, may hold values from -6 to 6
- exit_layer: int32 [48], P(('batch', 'seq')), parts along dimension 0, may hold values from 0 to 1
- tile_order: int32 [48], P('batch'), parts along dimension 0, may hold values from 0 to 11, each once
Outputs:
- attended: bfloat16 [1, 6144, 2048], P(None, ('batch', 'seq'), 'head'), parts along dimension 1
- live_tiles: int32 [4], P('batch'), parts along dimension 0
There are 4 independent parts, one for each index of `batch`. A program takes and returns all parts, laid end to end along the dimension named above; each array names one. Nothing has to cross between parts.
Inputs may be any that keep to these rules, and one draw needn't show every extreme that they name: Tile t covers tokens t * 128 to t * 128 + 127 of the token dimension; tile_order is a permutation of 0 to 11.
All inputs are finite; a program needn't handle non-finite values.
Results may differ from a plain program's by a relative error of at most 0.0049.
Values may be sent and summed in bfloat16 or wider, within the bound.
A program may use at most 128 MiB of HBM per device.

v0:
```python
import math

import jax
import jax.numpy as jnp
from jax import lax
from jax.sharding import PartitionSpec as P

HD = 256
TILE = 128


softcap = 50.0
query_scale = 0.0625


def lookup(lookup_table, wanted):
    table_slots = jnp.arange(lookup_table.shape[0], dtype=jnp.int32)
    picked = jnp.where(wanted[:, None] == table_slots[None, :], lookup_table[None, :], 0)
    return jnp.sum(picked, axis=1)


def token_positions(tile_order, first_row, row_count):
    offsets = first_row + jnp.arange(row_count, dtype=jnp.int32)
    return lookup(tile_order, offsets // TILE) * TILE + offsets % TILE


def attend(carried, key_rows, value_rows, key_pos, grouped, query_pos):
    row_count = key_rows.shape[0]
    kv_here = grouped.shape[1]
    block_rows = math.gcd(row_count, 512)
    key_heads = key_rows.reshape(row_count, kv_here, HD)
    value_heads = value_rows.reshape(row_count, kv_here, HD)

    def one_block(block_index, running):
        numerator, denominator = running
        lower_row = block_index * block_rows
        key_block = lax.dynamic_slice_in_dim(key_heads, lower_row, block_rows, 0)
        value_block = lax.dynamic_slice_in_dim(value_heads, lower_row, block_rows, 0)
        pos_block = lax.dynamic_slice_in_dim(key_pos, lower_row, block_rows, 0)
        scores = (
            jnp.einsum("tkgd,skd->kgts", grouped, key_block, preferred_element_type=jnp.float32)
            * query_scale
        )
        allowed = pos_block[None, :] <= query_pos[:, None]
        weights = jnp.where(allowed[None, None], jnp.exp(softcap * jnp.tanh(scores / softcap)), 0.0)
        denominator = denominator + jnp.sum(weights, axis=-1)
        numerator = numerator + jnp.einsum(
            "kgts,skd->kgtd",
            weights.astype(jnp.bfloat16),
            value_block,
            preferred_element_type=jnp.float32,
        )
        return (numerator, denominator)

    return lax.fori_loop(0, row_count // block_rows, one_block, carried)


def attend_live(carried, key_rows, value_rows, key_pos, grouped, query_pos):
    return attend(carried, key_rows, value_rows, key_pos, grouped, query_pos)


def finish(running, live_rows):
    numerator, denominator = running
    divisor = jnp.where(denominator > 0.0, denominator, 1.0)
    output = numerator / divisor[..., None]
    row_count = output.shape[2]
    output = jnp.transpose(output, (2, 0, 1, 3)).reshape(row_count, -1)
    return jnp.where(live_rows[:, None], output, 0.0).astype(jnp.bfloat16)


def body(queries, keys, values, exit_layer, tile_order):
    layer_count, row_count, q_width = queries.shape
    kv_here = keys.shape[2] // HD
    heads_here = q_width // HD
    group_size = heads_here // kv_here
    my_index = lax.axis_index("seq")
    first_row = my_index * row_count
    query_pos = token_positions(tile_order, first_row, row_count)
    token_exits = jnp.repeat(exit_layer, TILE, total_repeat_length=row_count)
    grouped = queries.reshape(layer_count, row_count, kv_here, group_size, HD)
    empty = (
        jnp.zeros((kv_here, group_size, row_count, HD), jnp.float32),
        jnp.zeros((kv_here, group_size, row_count), jnp.float32),
    )
    live_flags = [token_exits > 0]
    layer_id = 0
    any_live = jnp.any(live_flags[layer_id])

    def fold_one(carried, pieces, begin_at, layer_id=layer_id, any_live=any_live):
        key_pos = token_positions(tile_order, begin_at, pieces[0].shape[0])
        return attend_live(carried, pieces[0], pieces[1], key_pos, grouped[layer_id], query_pos)

    results = fold_one(
        empty,
        (
            lax.all_gather(keys[layer_id], "seq", axis=0, tiled=True),
            lax.all_gather(values[layer_id], "seq", axis=0, tiled=True),
        ),
        jnp.int32(0),
    )
    attended = jnp.stack([finish(results, live_flags[0])])
    local_counts = jnp.stack([jnp.sum((exit_layer > 0).astype(jnp.int32))])
    live_tiles = lax.psum(local_counts, "seq")
    return (attended, live_tiles)


def solution(mesh):
    return jax.shard_map(
        body,
        mesh=mesh,
        in_specs=(
            P(None, ("batch", "seq"), "head"),
            P(None, ("batch", "seq"), "head"),
            P(None, ("batch", "seq"), "head"),
            P(("batch", "seq")),
            P("batch"),
        ),
        out_specs=(P(None, ("batch", "seq"), "head"), P("batch")),
        check_vma=False,
    )
```

profile of v0, /device:TPU:0, one launch (start us, length us, event | category | flops | bytes accessed | tf_op | source)
XLA Modules:
  0.0 120.0 jit_solution(592446939675745330)
XLA Ops:
  7.2 2.0 %copy.18 = bf16[1,384,512]{1,2,0:T(8,128)(2,1)} copy(bf16[1,384,512]{2,1,0:T(8,128)(2,1)} %param.10) | data formatting | bytes 786432 | tf_op args[1]
  9.3 1.9 %copy.20 = bf16[1,384,512]{1,2,0:T(8,128)(2,1)} copy(bf16[1,384,512]{2,1,0:T(8,128)(2,1)} %param.11) | data formatting | bytes 786432 | tf_op args[2]
  11.2 0.6 fusion.37
  11.9 10.6 %psum.7 = s32[1]{0:T(128)} all-reduce(s32[1]{0:T(128)} %bitcast.9), channel_id=1, replica_groups=mesh['batch'=4,'seq'=4,'head'=2] {'seq'}, use_global_device_ids=true, to_apply=%region_6.7 | all-reduce | flops 1 | bytes 8 | tf_op jit(solution)/shard_map/psum | solution.py:103
  22.4 0.4 copy.19
  22.8 0.3 copy.22
  23.1 0.7 fusion.38
  23.8 2.0 %fusion.35 = s32[384]{0:T(512)S(1)} fusion(s32[1,1,3,128]{3,2,1,0:T(4,128)S(1)} %get-tuple-element.280, s32[1,1,3,128]{3,2,1,0:T(4,128)S(1)} %get-tuple-element.279, s32[]{:T(128)} %bitcast.2, s32[]{:T(128)} %bitcast.4, s32[]{:T(128)} %bitcast.3), kind=kLoop, calls=%fused_computation.61 | loop fusion | flops 2304 | bytes 4620 | tf_op jit(solution)/shard_map/jit(_take)/gather | solution.py:79
  26.0 23.5 %all-gather.5.cloned.1.call-done = bf16[1,1536,512]{1,2,0:T(8,128)(2,1)} async-done(((bf16[1,384,512]{1,2,0:T(8,128)(2,1)}), bf16[1,1536,512]{1,2,0:T(8,128)(2,1)}) %all-gather.5.cloned.1.call-update) | async-done | bytes 1572880 | tf_op jit(solution)/shard_map/all_gather | solution.py:96
  49.5 37.5 %all-gather.7.cloned.1.call-done = bf16[1,1536,512]{1,2,0:T(8,128)(2,1)} async-done(((bf16[1,384,512]{1,2,0:T(8,128)(2,1)}), bf16[1,1536,512]{1,2,0:T(8,128)(2,1)}) %all-gather.7.cloned.1.call-update) | async-done | bytes 1572880 | tf_op jit(solution)/shard_map/all_gather | solution.py:97
  87.0 23.4 %while.19 = (s32[]{:T(128)}, f32[2,2,384,256]{3,2,1,0:T(8,128)S(1)}, f32[2,2,384]{2,1,0:T(2,128)S(1)}, s32[1536]{0:T(1024)S(1)}, s32[384]{0:T(512)S(1)}, /*index...) while((s32[]{:T(128)}, ...), condition=%wide.region_4.5_spmd.clone, body=%wide.region_2.4_spmd.clone.sunk | while | flops 812582400 | bytes 11894466 | solution.py:55
  87.1 0.2 broadcast_compare_fusion.2
  87.3 3.9 %fusion.47 = (f32[2,2,384]{2,1,0:T(2,128)S(1)}, f32[2,512,384,2]{2,1,3,0:T(8,128)}) fusion(pred[384,512]{0,1:T(8,128)(4,1)S(1)} %broadcast_compare_fusion.2, bf16[384,2,2,256]{3,0,2,1:T(8,128)(2,1)S(1)} %get-tuple-element.364, bf16[1536,2,256]{0,2,1:T(8,128)(2,1)} %get-tuple-element.363, s32[]{:T(128)S(6)} %select_n.150), kind=kOutput, calls=%fused_computation.1.clone.1 | convolution fusion | flops 405797376 | bytes 4659204 | tf_op jit(solution)/shard_map/while/body/eval_jaxpr/tkgd,skd->kgts/dot_general | solution.py:41
  91.2 3.6 %select_add_fusion.4 = f32[2,2,384,256]{3,2,1,0:T(8,128)S(1)} fusion(f32[2,2,384,256]{3,2,1,0:T(8,128)S(1)} %get-tuple-element.347, f32[2,512,384,2]{2,1,3,0:T(8,128)} %get-tuple-element.332, pred[384,512]{0,1:T(8,128)(4,1)S(1)} %broadcast_compare_fusion.2, pred[]{:T(512)S(6)} %compare.35, bf16[1536,2,256]{0,2,1:T(8,128)(2,1)} %get-tuple-element.365, ...), kind=kOutput, calls=%fused_computation.4.clone.1 | convolution fusion | flops 406585344 | bytes 7012357 | tf_op jit(solution)/shard_map/while/body/eval_jaxpr/kgts,skd->kgtd/dot_general | solution.py:47
  94.9 0.2 broadcast_compare_fusion.2
  95.1 3.9 %fusion.47 = (f32[2,2,384]{2,1,0:T(2,128)S(1)}, f32[2,512,384,2]{2,1,3,0:T(8,128)}) fusion(pred[384,512]{0,1:T(8,128)(4,1)S(1)} %broadcast_compare_fusion.2, bf16[384,2,2,256]{3,0,2,1:T(8,128)(2,1)S(1)} %get-tuple-element.364, bf16[1536,2,256]{0,2,1:T(8,128)(2,1)} %get-tuple-element.363, s32[]{:T(128)S(6)} %select_n.150), kind=kOutput, calls=%fused_computation.1.clone.1 | convolution fusion | flops 405797376 | bytes 4659204 | tf_op jit(solution)/shard_map/while/body/eval_jaxpr/tkgd,skd->kgts/dot_general | solution.py:41
  99.0 3.6 %select_add_fusion.4 = f32[2,2,384,256]{3,2,1,0:T(8,128)S(1)} fusion(f32[2,2,384,256]{3,2,1,0:T(8,128)S(1)} %get-tuple-element.347, f32[2,512,384,2]{2,1,3,0:T(8,128)} %get-tuple-element.332, pred[384,512]{0,1:T(8,128)(4,1)S(1)} %broadcast_compare_fusion.2, pred[]{:T(512)S(6)} %compare.35, bf16[1536,2,256]{0,2,1:T(8,128)(2,1)} %get-tuple-element.365, ...), kind=kOutput, calls=%fused_computation.4.clone.1 | convolution fusion | flops 406585344 | bytes 7012357 | tf_op jit(solution)/shard_map/while/body/eval_jaxpr/kgts,skd->kgtd/dot_general | solution.py:47
  102.7 0.2 broadcast_compare_fusion.2
  102.9 3.9 %fusion.47 = (f32[2,2,384]{2,1,0:T(2,128)S(1)}, f32[2,512,384,2]{2,1,3,0:T(8,128)}) fusion(pred[384,512]{0,1:T(8,128)(4,1)S(1)} %broadcast_compare_fusion.2, bf16[384,2,2,256]{3,0,2,1:T(8,128)(2,1)S(1)} %get-tuple-element.364, bf16[1536,2,256]{0,2,1:T(8,128)(2,1)} %get-tuple-element.363, s32[]{:T(128)S(6)} %select_n.150), kind=kOutput, calls=%fused_computation.1.clone.1 | convolution fusion | flops 405797376 | bytes 4659204 | tf_op jit(solution)/shard_map/while/body/eval_jaxpr/tkgd,skd->kgts/dot_general | solution.py:41
  106.8 3.6 %select_add_fusion.4 = f32[2,2,384,256]{3,2,1,0:T(8,128)S(1)} fusion(f32[2,2,384,256]{3,2,1,0:T(8,128)S(1)} %get-tuple-element.347, f32[2,512,384,2]{2,1,3,0:T(8,128)} %get-tuple-element.332, pred[384,512]{0,1:T(8,128)(4,1)S(1)} %broadcast_compare_fusion.2, pred[]{:T(512)S(6)} %compare.35, bf16[1536,2,256]{0,2,1:T(8,128)(2,1)} %get-tuple-element.365, ...), kind=kOutput, calls=%fused_computation.4.clone.1 | convolution fusion | flops 406585344 | bytes 7012357 | tf_op jit(solution)/shard_map/while/body/eval_jaxpr/kgts,skd->kgtd/dot_general | solution.py:47
  110.4 0.3 divide_bitcast_fusion
  110.7 0.8 copy.24
  111.5 0.6 reshape.199
  112.1 1.1 select_convert_fusion
  (27 shorter events, 0.6 us)
Async XLA Ops:
  7.2 4.1 %copy-start.1 = (s32[3]{0:T(128)S(1)}, s32[3]{0:T(128)}, u32[]{:S(2)}) copy-start(s32[3]{0:T(128)} %param.12) | copy-start | bytes 40
  7.2 15.2 %copy-start = (bf16[1,384,1024]{2,1,0:T(8,128)(2,1)S(1)}, bf16[1,384,1024]{2,1,0:T(8,128)(2,1)}, u32[]{:S(2)}) copy-start(bf16[1,384,1024]{2,1,0:T(8,128)(2,1)} %param.9) | copy-start | bytes 2359300
  7.2 42.3 %all-gather.5.cloned.1.call-start = ((), (), s32[]{:S(2)}) async-start(), calls=%async_computation | async-start | bytes 1966080 | tf_op jit(solution)/shard_map/all_gather | solution.py:96
  9.2 77.8 %all-gather.7.cloned.1.call-start = ((), (), s32[]{:S(2)}) async-start(), calls=%async_computation.1 | async-start | bytes 1966080 | tf_op jit(solution)/shard_map/all_gather | solution.py:97
  22.4 3.3 %copy-start.2 = (s32[12]{0:T(128)S(1)}, s32[12]{0:T(128)}, u32[]{:S(2)}) copy-start(s32[12]{0:T(128)} %param.13) | copy-start | bytes 148
Sparse Core Ops, SparseCore 0:
  10.1 39.3 all-gather.4
  51.1 35.9 all-gather.6
where the time goes:
time: 120 us
  waiting for transfers between devices  61.1 us (51%)
  matrix products  22.5 us (19%)
  between operations  14.2 us (12%)
  blocking collectives  10.6 us (9%)
  local copies, waits for them, and re-layouts  6.8 us (6%)
  other arithmetic  4.74 us (4%)
    all_gather x1, waiting for transfers between devices, body(): lax.all_gather(values[layer_id], 'seq', axis=0, tiled=True)  37.5 us
    all_gather x1, waiting for transfers between devices, body(): lax.all_gather(keys[layer_id], 'seq', axis=0, tiled=True)  23.5 us
    dot_general x3, matrix products, one_block(): jnp.einsum('tkgd,skd->kgts', grouped, key_block, preferred_element_type=j...  11.8 us
    dot_general x3, matrix products, one_block(): jnp.einsum('kgts,skd->kgtd', weights.astype(jnp.bfloat16), value_block, p...  10.7 us
    psum x1, blocking collectives, body(): live_tiles = lax.psum(local_counts, 'seq')  10.6 us
    unnamed x10, local copies, waits for them, and re-layouts  4.53 us
  transfers between devices with their start and end apart: 2, of which 2 were waited for; matrix products, arithmetic and copies ran while one was open for 5% of the time, Pallas kernels for 0%

commit v1 on v0

v1 whole, which is shorter than its diff:
```python
import functools
import math

import jax
import jax.numpy as jnp
from jax import lax
from jax.experimental import pallas as pl
from jax.experimental.pallas import tpu as pltpu
from jax.sharding import PartitionSpec as P

HD = 256
TILE = 128
SOFTCAP = 50.0
QUERY_SCALE = 0.0625
IN_SCALE = QUERY_SCALE / SOFTCAP
OUT_SCALE = SOFTCAP * math.log2(math.e)
MESH = pl.DeviceIdType.MESH


def kernel(
    n, order_ref, exit_ref, exits_vec, q_hbm, k_hbm, v_hbm, out_ref, live_ref,
    q_ref, kv, acc, den, exits, in_sem, send_sem, recv_sem, exit_send, exit_recv,
):
    me = lax.axis_index("seq")
    tiles = kv.shape[1]
    rows, q_width = q_ref.shape
    heads = q_width // HD
    group = heads // (k_hbm.shape[1] // HD)

    q_copy = pltpu.make_async_copy(q_hbm, q_ref, in_sem.at[2 * tiles])

    def own_copy(t, which):
        src = (k_hbm, v_hbm)[which]
        return pltpu.make_async_copy(
            src.at[pl.ds(t * TILE, TILE)], kv.at[me, t, which], in_sem.at[2 * t + which]
        )

    for t in range(tiles):
        for which in range(2):
            own_copy(t, which).start()
    q_copy.start()

    barrier = pltpu.get_barrier_semaphore()
    for d in range(1, n):
        pl.semaphore_signal(
            barrier, inc=1, device_id={"seq": lax.rem(me + d, n)}, device_id_type=MESH
        )
    pl.semaphore_wait(barrier, n - 1)

    def hop(owner, t, way):
        step = 1 if way == 0 else -1
        return pltpu.make_async_remote_copy(
            src_ref=kv.at[owner, t],
            dst_ref=kv.at[owner, t],
            send_sem=send_sem.at[way, owner, t],
            recv_sem=recv_sem.at[owner, t],
            device_id={"seq": jnp.clip(me + step, 0, n - 1)},
            device_id_type=MESH,
        )

    def can(way):
        return me < n - 1 if way == 0 else me > 0

    for t in range(tiles):
        for which in range(2):
            own_copy(t, which).wait()
        for way in range(2):
            @pl.when(can(way))
            def _():
                hop(me, t, way).start()

    def exit_copy(d):
        return pltpu.make_async_remote_copy(
            src_ref=exits_vec,
            dst_ref=exits.at[d - 1],
            send_sem=exit_send.at[d - 1],
            recv_sem=exit_recv.at[d - 1],
            device_id={"seq": lax.rem(me + d, n)},
            device_id_type=MESH,
        )

    for d in range(1, n):
        exit_copy(d).start()

    acc[...] = jnp.zeros_like(acc)
    den[...] = jnp.zeros_like(den)
    q_copy.wait()
    ahead = lax.broadcasted_iota(jnp.int32, (TILE, TILE), 1) - lax.broadcasted_iota(
        jnp.int32, (TILE, TILE), 0
    )

    def fold(owner, t):
        key_place = order_ref[owner * tiles + t]
        for i in range(rows // TILE):
            here = pl.ds(i * TILE, TILE)
            reach = (order_ref[me * tiles + i] - key_place) * TILE
            allowed = ahead <= reach
            for h in range(heads):
                cols = pl.ds(h * HD, HD)
                kv_cols = pl.ds((h // group) * HD, HD)
                scores = lax.dot_general(
                    q_ref[here, cols], kv[owner, t, 0, :, kv_cols],
                    (((1,), (1,)), ((), ())), preferred_element_type=jnp.float32,
                )
                weights = jnp.where(
                    allowed, jnp.exp2(OUT_SCALE * jnp.tanh(scores * IN_SCALE)), 0.0
                )
                den[h, here, :] += weights
                acc[here, cols] += jnp.dot(
                    weights.astype(jnp.bfloat16), kv[owner, t, 1, :, kv_cols],
                    preferred_element_type=jnp.float32,
                )

    @pl.loop(0, tiles)
    def _(t):
        fold(me, t)

    @pl.loop(1, n)
    def _(s):
        @pl.loop(0, tiles)
        def _(t):
            for way in range(2):
                owner = me - s if way == 0 else me + s

                @pl.when(owner >= 0 if way == 0 else owner < n)
                def _():
                    hop(owner, t, way).wait_recv()

                    @pl.when(can(way))
                    def _():
                        hop(owner, t, way).start()

            for way in range(2):
                owner = me - s if way == 0 else me + s

                @pl.when(owner >= 0 if way == 0 else owner < n)
                def _():
                    fold(owner, t)

    for i in range(rows // TILE):
        here = pl.ds(i * TILE, TILE)
        is_live = exit_ref[i] > 0
        for h in range(heads):
            cols = pl.ds(h * HD, HD)
            total = jnp.sum(den[h, here, :], axis=1, keepdims=True)
            result = acc[here, cols] / total
            out_ref[here, cols] = jnp.where(is_live, result, 0.0).astype(out_ref.dtype)

    count = jnp.sum((exits_vec[...] > 0).astype(jnp.int32))
    for d in range(1, n):
        exit_copy(d).wait()
        count += jnp.sum((exits[d - 1] > 0).astype(jnp.int32))
    live_ref[0] = count

    @pl.loop(0, n)
    def _(s):
        @pl.loop(0, tiles)
        def _(t):
            for way in range(2):
                owner = me - s if way == 0 else me + s

                @pl.when((owner >= 0 if way == 0 else owner < n) & can(way))
                def _():
                    hop(owner, t, way).wait_send()


def body(n, queries, keys, values, exit_layer, tile_order):
    rows, q_width = queries.shape[1:]
    kv_width = keys.shape[2]
    tiles = rows // TILE
    heads = q_width // HD
    exits_vec = jnp.pad(exit_layer, (0, TILE - tiles)).reshape(1, TILE)
    smem = pl.BlockSpec(memory_space=pltpu.SMEM)
    hbm = pl.BlockSpec(memory_space=pl.ANY)
    vmem = pl.BlockSpec(memory_space=pltpu.VMEM)
    attended, live = pl.pallas_call(
        functools.partial(kernel, n),
        out_shape=(
            jax.ShapeDtypeStruct((rows, q_width), jnp.bfloat16),
            jax.ShapeDtypeStruct((1,), jnp.int32),
        ),
        in_specs=[smem, smem, vmem, hbm, hbm, hbm],
        out_specs=(vmem, smem),
        scratch_shapes=[
            pltpu.VMEM((rows, q_width), jnp.bfloat16),
            pltpu.VMEM((n, tiles, 2, TILE, kv_width), jnp.bfloat16),
            pltpu.VMEM((rows, q_width), jnp.float32),
            pltpu.VMEM((heads, rows, TILE), jnp.float32),
            pltpu.VMEM((n - 1, 1, TILE), jnp.int32),
            pltpu.SemaphoreType.DMA((2 * tiles + 1,)),
            pltpu.SemaphoreType.DMA((2, n, tiles)),
            pltpu.SemaphoreType.DMA((n, tiles)),
            pltpu.SemaphoreType.DMA((n - 1,)),
            pltpu.SemaphoreType.DMA((n - 1,)),
        ],
        compiler_params=pltpu.CompilerParams(collective_id=0, has_side_effects=True),
        name="attend_line",
    )(tile_order, exit_layer, exits_vec, queries[0], keys[0], values[0])
    return attended[None], live


def solution(mesh):
    return jax.shard_map(
        functools.partial(body, mesh.shape["seq"]),
        mesh=mesh,
        in_specs=(
            P(None, ("batch", "seq"), "head"),
            P(None, ("batch", "seq"), "head"),
            P(None, ("batch", "seq"), "head"),
            P(("batch", "seq")),
            P("batch"),
        ),
        out_specs=(P(None, ("batch", "seq"), "head"), P("batch")),
        check_vma=False,
    )
```

time: 120 us -> 66.2 us (0.55)
  waiting for transfers between devices: 61.1 us -> 0 us
  Pallas kernels: 0 us -> 60.3 us
  matrix products: 22.5 us -> 0 us
  between operations: 14.2 us -> 2.41 us
  blocking collectives: 10.6 us -> 0 us
  other arithmetic: 4.74 us -> 0 us
  local copies, waits for them, and re-layouts: 6.8 us -> 3.23 us
    all_gather x2 -> x0, waiting for transfers between devices: 61.1 us -> none  [the longest x1 37.5 us: body(): lax.all_gather(values[layer_id], 'seq', axis=0, tiled=True)]
    pallas_call x0 -> x1, Pallas kernels: none -> 60.3 us  [body(): pl.pallas_call(functools.partial(kernel, n), out_shape=(jax.ShapeDtypeStr...]
    dot_general x6 -> x0, matrix products: 22.5 us -> none  [the longest x3 11.8 us: one_block(): jnp.einsum('tkgd,skd->kgts', grouped, key_block, preferred_element_type=j...]
    psum x1 -> x0, blocking collectives: 10.6 us -> none  [body(): live_tiles = lax.psum(local_counts, 'seq')]
    gather x1 -> x0, other arithmetic: 1.95 us -> none  [body(): token_exits = jnp.repeat(exit_layer, TILE, total_repeat_length=row_count)]
    unnamed x10 -> x3, local copies, waits for them, and re-layouts: 4.53 us -> 2.71 us
  transfers between devices with their start and end apart: 2 -> 0, of which waited for: 2 -> 0; matrix products, arithmetic and copies ran while one was open for 5% -> 0% of each run, Pallas kernels for 0% -> 0%
where the time goes in v1:
time: 66.2 us; the launch traced here: 66 us
  Pallas kernels  60.3 us (91%)
  local copies, waits for them, and re-layouts  3.23 us (5%)
  between operations  2.41 us (4%)
    pallas_call x1, Pallas kernels, body(): pl.pallas_call(functools.partial(kernel, n), out_shape=(jax.ShapeDtypeStr...  60.3 us
    unnamed x3, local copies, waits for them, and re-layouts  2.71 us

profile of v1, /device:TPU:0, one launch (start us, length us, event | category | flops | bytes accessed | tf_op | source)
XLA Modules:
  0.0 66.0 jit_solution(1370049238660756371)
XLA Ops:
  0.6 0.0 copy-start
  0.6 0.6 copy-done
  1.3 0.5 pad_bitcast_fusion.exits_vec
  1.8 60.3 %attend_line.1 = (bf16[384,1024]{1,0:T(8,128)(2,1)}, s32[1]{0:T(128)}) custom-call(s32[12]{0:T(128)} %order_ref.1, s32[3]{0:T(128)} %exit_ref.1, s32[1,128]{1,0:T(1,128)} %pad_bitcast_fusion.exits_vec, bf16[384,1024]{1,0:T(8,128)(2,1)} %bitcast.6, bf16[384,512]{1,0:T(8,128)(2,1)} %bitcast.8, bf16[384,512]{1,0:T(8,128)(2,1)} %bitcast.9), custom_call_target="tpu_custom_call" | custom-call | tf_op jit(solution)/shard_map/attend_line/pallas_call | solution.py:176
  62.1 2.1 %copy.9 = bf16[1,384,1024]{2,1,0:T(8,128)(2,1)} copy(bf16[1,384,1024]{2,1,0:T(8,128)(2,1)} %bitcast.7) | data formatting | bytes 1572864
Async XLA Ops:
  0.6 0.7 copy-start

commit v2 on v1

v2 whole, which is shorter than its diff:
```python
import functools
import math

import jax
import jax.numpy as jnp
from jax import lax
from jax.experimental import pallas as pl
from jax.experimental.pallas import tpu as pltpu
from jax.sharding import PartitionSpec as P

HD = 256
TILE = 128
SOFTCAP = 50.0
QUERY_SCALE = 0.0625
IN_SCALE = QUERY_SCALE / SOFTCAP
OUT_SCALE = SOFTCAP * math.log2(math.e)
MESH = pl.DeviceIdType.MESH


def kernel(
    n, order_ref, exits_vec, q_hbm, k_hbm, v_hbm, out_ref, live_ref,
    qb, kv, acc, den, done, exits, kv_sem, q_sem, send_sem, recv_sem,
    q_send, q_recv, o_send, o_recv, exit_send, exit_recv,
):
    me = lax.axis_index("seq")
    core = lax.axis_index("head")
    tiles = kv.shape[2]
    rows, q_half = qb.shape[1:]
    kv_half = kv.shape[5]
    heads = q_half // HD
    group = heads // (kv_half // HD)
    at_end = (me == 0) | (me == n - 1)
    serves = (me == 1) | (me == n - 2)
    end = jnp.where(me < n // 2, 0, n - 1)
    inward = jnp.where(me < n // 2, 1, -1)

    def peer(step):
        return {"seq": jnp.clip(me + step, 0, n - 1)}

    def own_copy(hh, t, which):
        src = (k_hbm, v_hbm)[which]
        return pltpu.make_async_copy(
            src.at[pl.ds(t * TILE, TILE), pl.ds(pl.multiple_of(hh * kv_half, kv_half), kv_half)],
            kv.at[me, hh, t, which],
            kv_sem.at[hh, t, which],
        )

    def own_queries(hh):
        return pltpu.make_async_copy(
            q_hbm.at[:, pl.ds(hh * q_half, q_half)], qb.at[hh], q_sem.at[hh]
        )

    first = core
    for hh in (first, 1 - first):
        for t in range(tiles):
            for which in range(2):
                own_copy(hh, t, which).start()
    for hh in range(2):
        own_queries(hh).start()

    barrier = pltpu.get_barrier_semaphore()
    for d in range(1, n):
        pl.semaphore_signal(
            barrier, inc=1, device_id={"seq": lax.rem(me + d, n)}, device_id_type=MESH
        )
    pl.semaphore_wait(barrier, n - 1)

    def hop(owner, hh, t, step):
        return pltpu.make_async_remote_copy(
            src_ref=kv.at[owner, hh, t],
            dst_ref=kv.at[owner, hh, t],
            send_sem=send_sem.at[(step + 1) // 2, owner, hh, t],
            recv_sem=recv_sem.at[owner, hh, t],
            device_id=peer(step),
            device_id_type=MESH,
        )

    def goes(hh, step):
        room = jnp.where(step > 0, n - 1 - me, me)
        return (room > 1) | ((room == 1) & (hh == 1))

    def send(owner, hh, t, step):
        @pl.when(goes(hh, step))
        def _():
            hop(owner, hh, t, step).start()

    def query_copy(t):
        part = pl.ds(t * TILE, TILE)
        return pltpu.make_async_remote_copy(
            src_ref=qb.at[0, part], dst_ref=qb.at[2, part],
            send_sem=q_send.at[t], recv_sem=q_recv.at[t],
            device_id=peer(inward), device_id_type=MESH,
        )

    def done_copy(t):
        part = pl.ds(t * TILE, TILE)
        return pltpu.make_async_remote_copy(
            src_ref=done.at[0, part], dst_ref=done.at[1, part],
            send_sem=o_send.at[t], recv_sem=o_recv.at[t],
            device_id=peer(-inward), device_id_type=MESH,
        )

    for t in range(tiles):
        for which in range(2):
            own_copy(first, t, which).wait()
        send(me, first, t, inward)
        send(me, first, t, -inward)
        if t == 0:
            own_queries(0).wait()

        @pl.when(at_end)
        def _():
            query_copy(t).start()

    def exit_copy(d):
        return pltpu.make_async_remote_copy(
            src_ref=exits_vec, dst_ref=exits.at[d - 1],
            send_sem=exit_send.at[d - 1], recv_sem=exit_recv.at[d - 1],
            device_id={"seq": lax.rem(me + d, n)}, device_id_type=MESH,
        )

    for t in range(tiles):
        for which in range(2):
            own_copy(1 - first, t, which).wait()
        send(me, 1 - first, t, -inward)

        @pl.when(at_end)
        def _():
            send(me, 1 - first, t, inward)

    for d in range(1, n):
        exit_copy(d).start()

    acc[...] = jnp.zeros_like(acc)
    den[...] = jnp.zeros_like(den)
    own_queries(1).wait()
    ahead = lax.broadcasted_iota(jnp.int32, (TILE, TILE), 1) - lax.broadcasted_iota(
        jnp.int32, (TILE, TILE), 0
    )

    def fold_into(slot, row_owner, owner, hh, t):
        key_place = order_ref[owner * tiles + t]
        for i in range(rows // TILE):
            here = pl.ds(i * TILE, TILE)
            reach = (order_ref[row_owner * tiles + i] - key_place) * TILE
            allowed = ahead <= reach
            for h in range(heads):
                cols = pl.ds(h * HD, HD)
                kv_cols = pl.ds((h // group) * HD, HD)
                scores = lax.dot_general(
                    qb[slot, here, cols], kv[owner, hh, t, 0, :, kv_cols],
                    (((1,), (1,)), ((), ())), preferred_element_type=jnp.float32,
                )
                weights = jnp.where(
                    allowed, jnp.exp2(OUT_SCALE * jnp.tanh(scores * IN_SCALE)), 0.0
                )
                den[slot, h, here, :] += weights
                acc[slot, here, cols] += jnp.dot(
                    weights.astype(jnp.bfloat16), kv[owner, hh, t, 1, :, kv_cols],
                    preferred_element_type=jnp.float32,
                )

    def fold(owner, hh, t, phase):
        low = jnp.where(at_end & (hh == 0), 1, 0)
        high = jnp.where(serves & (hh == 0) & (phase == 1), 2, 1)

        @pl.loop(low, high)
        def _(k):
            fold_into(
                jnp.where(k == 0, hh, 2), jnp.where(k == 0, me, end), owner, hh, t
            )

    def finish(slot, i, h):
        here = pl.ds(i * TILE, TILE)
        total = jnp.sum(den[slot, h, here, :], axis=1, keepdims=True)
        return (acc[slot, here, pl.ds(h * HD, HD)] / total).astype(jnp.bfloat16)

    def finish_served():
        for t in range(tiles):
            for h in range(heads):
                done[0, pl.ds(t * TILE, TILE), pl.ds(h * HD, HD)] = finish(2, t, h)
            if t > 0:
                done_copy(t - 1).start()

    def arrive(owner, hh, t, side, phase):
        @pl.when((owner >= 0) & (owner < n) & ~(at_end & (hh == 0)))
        def _():
            hop(owner, hh, t, side).wait_recv()
            send(owner, hh, t, -side)

    def take(owner, hh, t, phase):
        @pl.when((owner >= 0) & (owner < n) & ~(at_end & (hh == 0)))
        def _():
            fold(owner, hh, t, phase)

    near = []
    for s in (1, 2):
        for t in range(tiles):
            near.append((tiles * (s - 1) + t + 1.0, 1, s, t))
            if s == 1 or n > 4:
                near.append((tiles * 2 * (s - 1) + 2 * t + 1.1, -1, s, t))
    near.sort()

    @pl.loop(0, 2)
    def _(phase):
        hh = jnp.where(phase == 0, first, 1 - first)

        @pl.when(serves & (hh == 0) & (phase == 1))
        def _():
            for t in range(tiles):
                query_copy(t).wait_recv()

        @pl.loop(0, tiles)
        def _(t):
            fold(me, hh, t, phase)

        for _, sign, s, t in near:
            side = inward * sign
            owner = me + side * s
            arrive(owner, hh, t, side, phase)
            if sign == -1 and s == 1:
                @pl.when((phase == 0) & ~at_end)
                def _():
                    send(me, 1 - first, t, inward)
            take(owner, hh, t, phase)

        @pl.loop(3, n)
        def _(s):
            @pl.loop(0, tiles)
            def _(t):
                for sign in (1, -1) if n > 4 else (1,):
                    side = inward * sign
                    arrive(me + side * s, hh, t, side, phase)
                    take(me + side * s, hh, t, phase)

        @pl.when(serves & (hh == 0))
        def _():
            @pl.when(phase == 0)
            def _():
                for t in range(tiles):
                    query_copy(t).wait_recv()

                @pl.loop(0, n)
                def _(owner):
                    @pl.loop(0, tiles)
                    def _(t):
                        fold_into(2, end, owner, 0, t)

            finish_served()
            for h in range(heads):
                out_ref[pl.ds(0, TILE), pl.ds(h * HD, HD)] = finish(0, 0, h)
            done_copy(tiles - 1).start()

    for i in range(rows // TILE):
        for h in range(heads):
            out_ref[pl.ds(i * TILE, TILE), pl.ds(q_half + h * HD, HD)] = finish(1, i, h)

    @pl.when(~at_end)
    def _():
        for i in range(rows // TILE):
            for h in range(heads):
                out_ref[pl.ds(i * TILE, TILE), pl.ds(h * HD, HD)] = finish(0, i, h)

    count = jnp.sum((exits_vec[...] > 0).astype(jnp.int32))
    for d in range(1, n):
        exit_copy(d).wait()
        count += jnp.sum((exits[d - 1] > 0).astype(jnp.int32))
    live_ref[0] = count

    @pl.when(at_end)
    def _():
        for t in range(tiles):
            here = pl.ds(t * TILE, TILE)
            done_copy(t).wait_recv()
            out_ref[here, pl.ds(0, q_half)] = done[1, here, :]
            query_copy(t).wait_send()

    @pl.when(serves)
    def _():
        for t in range(tiles):
            done_copy(t).wait_send()

    for step in (1, -1):
        @pl.loop(0, n)
        def _(s):
            owner = me - step * s

            @pl.loop(0, 2)
            def _(hh):
                @pl.when((owner >= 0) & (owner < n) & goes(hh, step))
                def _():
                    @pl.loop(0, tiles)
                    def _(t):
                        hop(owner, hh, t, step).wait_send()


def body(n, queries, keys, values, exit_layer, tile_order):
    rows, q_width = queries.shape[1:]
    kv_half = keys.shape[2] // 2
    q_half = q_width // 2
    tiles = rows // TILE
    exits_vec = jnp.pad(exit_layer, (0, TILE - tiles)).reshape(1, TILE)
    smem = pl.BlockSpec(memory_space=pltpu.SMEM)
    hbm = pl.BlockSpec(memory_space=pl.ANY)
    vmem = pl.BlockSpec(memory_space=pltpu.VMEM)
    dma = pltpu.SemaphoreType.DMA
    attended, live = pl.pallas_call(
        functools.partial(kernel, n),
        out_shape=(
            jax.ShapeDtypeStruct((rows, q_width), jnp.bfloat16),
            jax.ShapeDtypeStruct((1,), jnp.int32),
        ),
        in_specs=[smem, vmem, hbm, hbm, hbm],
        out_specs=(vmem, smem),
        scratch_shapes=[
            pltpu.VMEM((3, rows, q_half), jnp.bfloat16),
            pltpu.VMEM((n, 2, tiles, 2, TILE, kv_half), jnp.bfloat16),
            pltpu.VMEM((3, rows, q_half), jnp.float32),
            pltpu.VMEM((3, q_half // HD, rows, TILE), jnp.float32),
            pltpu.VMEM((2, rows, q_half), jnp.bfloat16),
            pltpu.VMEM((n - 1, 1, TILE), jnp.int32),
            dma((2, tiles, 2)),
            dma((2,)),
            dma((2, n, 2, tiles)),
            dma((n, 2, tiles)),
            dma((tiles,)),
            dma((tiles,)),
            dma((tiles,)),
            dma((tiles,)),
            dma((n - 1,)),
            dma((n - 1,)),
        ],
        compiler_params=pltpu.CompilerParams(collective_id=0, has_side_effects=True),
        name="attend_line",
    )(tile_order, exits_vec, queries[0], keys[0], values[0])
    live_rows = jnp.repeat(exit_layer > 0, TILE, total_repeat_length=rows)
    attended = jnp.where(live_rows[:, None], attended, jnp.zeros((), jnp.bfloat16))
    return attended[None], live


def solution(mesh):
    return jax.shard_map(
        functools.partial(body, mesh.shape["seq"]),
        mesh=mesh,
        in_specs=(
            P(None, ("batch", "seq"), "head"),
            P(None, ("batch", "seq"), "head"),
            P(None, ("batch", "seq"), "head"),
            P(("batch", "seq")),
            P("batch"),
        ),
        out_specs=(P(None, ("batch", "seq"), "head"), P("batch")),
        check_vma=False,
    )
```

time: 66.2 us -> 70 us (1.057)
  other arithmetic: 0 us -> 4.1 us
  local copies, waits for them, and re-layouts: 3.23 us -> 1.82 us
  Pallas kernels: 60.3 us -> 61.4 us
    broadcast_in_dim x0 -> x1, other arithmetic: none -> 2.14 us  [body(): return (attended[None], live)]
    unnamed x3 -> x2, local copies, waits for them, and re-layouts: 2.71 us -> 0.65 us
    gather x0 -> x1, other arithmetic: none -> 1.93 us  [body(): live_rows = jnp.repeat(exit_layer > 0, TILE, total_repeat_length=rows)]
    pallas_call x1, Pallas kernels: 60.3 us -> 61.4 us  [body(): pl.pallas_call(functools.partial(kernel, n), out_shape=(jax.ShapeDtypeStr...]
where the time goes in v2:
time: 70 us; the launch traced here: 69.7 us
  Pallas kernels  61.4 us (88%)
  other arithmetic  4.1 us (6%)
  between operations  2.42 us (3%)
  local copies, waits for them, and re-layouts  1.82 us (3%)
    pallas_call x1, Pallas kernels, body(): pl.pallas_call(functools.partial(kernel, n), out_shape=(jax.ShapeDtypeStr...  61.4 us
    broadcast_in_dim x1, other arithmetic, body(): return (attended[None], live)  2.14 us
    gather x1, other arithmetic, body(): live_rows = jnp.repeat(exit_layer > 0, TILE, total_repeat_length=rows)  1.93 us

profile of v2, /device:TPU:0, one launch (start us, length us, event | category | flops | bytes accessed | tf_op | source)
XLA Modules:
  0.0 69.7 jit_solution(5522857751774789958)
XLA Ops:
  0.6 0.0 copy-start
  0.6 0.6 copy-done
  1.3 0.5 pad_bitcast_fusion.exits_vec
  1.8 0.7 fusion.4
  2.5 1.9 %select_reduce_fusion = pred[384]{0:T(512)(128)(4,1)S(1)} fusion(pred[]{:T(512)} %bitcast.2, pred[]{:T(512)} %bitcast.4, pred[]{:T(512)} %bitcast.3, s32[1,1,3,128]{3,2,1,0:T(4,128)S(1)} %get-tuple-element.22, s32[1,1,3,128]{3,2,1,0:T(4,128)S(1)} %get-tuple-element.21), kind=kLoop, calls=%fused_computation.2 | loop fusion | flops 2304 | bytes 3459 | tf_op jit(solution)/shard_map/jit(_take)/gather | solution.py:336
  4.4 61.4 %attend_line.1 = (bf16[384,1024]{1,0:T(8,128)(2,1)}, s32[1]{0:T(128)}) custom-call(s32[12]{0:T(128)} %order_ref.1, s32[1,128]{1,0:T(1,128)} %pad_bitcast_fusion.exits_vec, bf16[384,1024]{1,0:T(8,128)(2,1)} %bitcast.32, bf16[384,512]{1,0:T(8,128)(2,1)} %bitcast.33, bf16[384,512]{1,0:T(8,128)(2,1)} %bitcast.34), custom_call_target="tpu_custom_call" | custom-call | tf_op jit(solution)/shard_map/attend_line/pallas_call | solution.py:307
  65.8 2.1 %select_bitcast_fusion = bf16[1,384,1024]{2,1,0:T(8,128)(2,1)} fusion(bf16[384,1024]{1,0:T(8,128)(2,1)} %get-tuple-element.16, pred[384]{0:T(512)(128)(4,1)S(1)} %and_select_fusion), kind=kLoop, calls=%fused_computation | loop fusion | flops 393216 | bytes 1573248 | tf_op jit(solution)/shard_map/broadcast_in_dim | solution.py:338
  (3 shorter events, 0.0 us)
Async XLA Ops:
  0.6 0.7 copy-start

commit v3 on v2

--- a/solution.py
+++ b/solution.py
@@ -18,17 +18,16 @@
 
 
 def kernel(
-    n, order_ref, exits_vec, q_hbm, k_hbm, v_hbm, out_ref, live_ref,
+    n, order_ref, exit_ref, exits_vec, q_hbm, k_hbm, v_hbm, out_ref, live_ref,
     qb, kv, acc, den, done, exits, kv_sem, q_sem, send_sem, recv_sem,
     q_send, q_recv, o_send, o_recv, exit_send, exit_recv,
 ):
     me = lax.axis_index("seq")
     core = lax.axis_index("head")
     tiles = kv.shape[2]
-    rows, q_half = qb.shape[1:]
+    heads, rows = qb.shape[1:3]
+    q_half = heads * HD
     kv_half = kv.shape[5]
-    heads = q_half // HD
-    group = heads // (kv_half // HD)
     at_end = (me == 0) | (me == n - 1)
     serves = (me == 1) | (me == n - 2)
     end = jnp.where(me < n // 2, 0, n - 1)
@@ -45,18 +44,20 @@
             kv_sem.at[hh, t, which],
         )
 
-    def own_queries(hh):
+    def own_queries(hh, h):
         return pltpu.make_async_copy(
-            q_hbm.at[:, pl.ds(hh * q_half, q_half)], qb.at[hh], q_sem.at[hh]
+            q_hbm.at[:, pl.ds(hh * q_half + h * HD, HD)], qb.at[hh, h], q_sem.at[hh, h]
         )
 
     first = core
+    for h in range(heads):
+        own_queries(0, h).start()
     for hh in (first, 1 - first):
         for t in range(tiles):
             for which in range(2):
                 own_copy(hh, t, which).start()
-    for hh in range(2):
-        own_queries(hh).start()
+    for h in range(heads):
+        own_queries(1, h).start()
 
     barrier = pltpu.get_barrier_semaphore()
     for d in range(1, n):
@@ -87,7 +88,7 @@
     def query_copy(t):
         part = pl.ds(t * TILE, TILE)
         return pltpu.make_async_remote_copy(
-            src_ref=qb.at[0, part], dst_ref=qb.at[2, part],
+            src_ref=qb.at[0, :, part], dst_ref=qb.at[2, :, part],
             send_sem=q_send.at[t], recv_sem=q_recv.at[t],
             device_id=peer(inward), device_id_type=MESH,
         )
@@ -100,16 +101,18 @@
             device_id=peer(-inward), device_id_type=MESH,
         )
 
+    for h in range(heads):
+        own_queries(0, h).wait()
+
     for t in range(tiles):
         for which in range(2):
             own_copy(first, t, which).wait()
         send(me, first, t, inward)
         send(me, first, t, -inward)
-        if t == 0:
-            own_queries(0).wait()
-
-        @pl.when(at_end)
-        def _():
+
+    @pl.when(at_end)
+    def _():
+        for t in range(tiles):
             query_copy(t).start()
 
     def exit_copy(d):
@@ -133,32 +136,33 @@
 
     acc[...] = jnp.zeros_like(acc)
     den[...] = jnp.zeros_like(den)
-    own_queries(1).wait()
+    for h in range(heads):
+        own_queries(1, h).wait()
     ahead = lax.broadcasted_iota(jnp.int32, (TILE, TILE), 1) - lax.broadcasted_iota(
         jnp.int32, (TILE, TILE), 0
     )
 
     def fold_into(slot, row_owner, owner, hh, t):
         key_place = order_ref[owner * tiles + t]
-        for i in range(rows // TILE):
-            here = pl.ds(i * TILE, TILE)
-            reach = (order_ref[row_owner * tiles + i] - key_place) * TILE
-            allowed = ahead <= reach
-            for h in range(heads):
-                cols = pl.ds(h * HD, HD)
-                kv_cols = pl.ds((h // group) * HD, HD)
-                scores = lax.dot_general(
-                    qb[slot, here, cols], kv[owner, hh, t, 0, :, kv_cols],
-                    (((1,), (1,)), ((), ())), preferred_element_type=jnp.float32,
-                )
-                weights = jnp.where(
-                    allowed, jnp.exp2(OUT_SCALE * jnp.tanh(scores * IN_SCALE)), 0.0
-                )
-                den[slot, h, here, :] += weights
-                acc[slot, here, cols] += jnp.dot(
-                    weights.astype(jnp.bfloat16), kv[owner, hh, t, 1, :, kv_cols],
-                    preferred_element_type=jnp.float32,
-                )
+        over = jnp.stack(
+            [
+                ahead - (order_ref[row_owner * tiles + i] - key_place) * TILE
+                for i in range(tiles)
+            ]
+        )
+        stacked = (heads * rows, HD)
+        scores = lax.dot_general(
+            qb[slot].reshape(stacked), kv[owner, hh, t, 0],
+            (((1,), (1,)), ((), ())), preferred_element_type=jnp.float32,
+        ).reshape(heads, tiles, TILE, TILE)
+        weights = jnp.where(
+            over[None] <= 0, jnp.exp2(OUT_SCALE * jnp.tanh(scores * IN_SCALE)), 0.0
+        ).reshape(heads * rows, TILE)
+        den[slot] += weights
+        acc[slot] += jnp.dot(
+            weights.astype(jnp.bfloat16), kv[owner, hh, t, 1],
+            preferred_element_type=jnp.float32,
+        )
 
     def fold(owner, hh, t, phase):
         low = jnp.where(at_end & (hh == 0), 1, 0)
@@ -171,9 +175,24 @@
             )
 
     def finish(slot, i, h):
-        here = pl.ds(i * TILE, TILE)
-        total = jnp.sum(den[slot, h, here, :], axis=1, keepdims=True)
-        return (acc[slot, here, pl.ds(h * HD, HD)] / total).astype(jnp.bfloat16)
+        here = pl.ds(h * rows + i * TILE, TILE)
+        total = jnp.sum(den[slot, here, :], axis=1, keepdims=True)
+        return (acc[slot, here, :] / total).astype(jnp.bfloat16)
+
+    def keep(slot, i, h):
+        out_ref[pl.ds(i * TILE, TILE), pl.ds(slot * q_half + h * HD, HD)] = live_only(
+            i, finish(slot, i, h)
+        )
+
+    def live_only(i, rows_out):
+        return jnp.where(exit_ref[i] > 0, rows_out, jnp.zeros_like(rows_out))
+
+    def late_fold(part, parts):
+        share = n * tiles // parts
+
+        @pl.loop(part * share, (part + 1) * share)
+        def _(k):
+            fold_into(2, end, k // tiles, 0, k % tiles)
 
     def finish_served():
         for t in range(tiles):
@@ -181,6 +200,9 @@
                 done[0, pl.ds(t * TILE, TILE), pl.ds(h * HD, HD)] = finish(2, t, h)
             if t > 0:
                 done_copy(t - 1).start()
+        for h in range(heads):
+            keep(0, 0, h)
+        done_copy(tiles - 1).start()
 
     def arrive(owner, hh, t, side, phase):
         @pl.when((owner >= 0) & (owner < n) & ~(at_end & (hh == 0)))
@@ -205,7 +227,7 @@
     def _(phase):
         hh = jnp.where(phase == 0, first, 1 - first)
 
-        @pl.when(serves & (hh == 0) & (phase == 1))
+        @pl.when(serves & (phase == 1))
         def _():
             for t in range(tiles):
                 query_copy(t).wait_recv()
@@ -213,16 +235,29 @@
         @pl.loop(0, tiles)
         def _(t):
             fold(me, hh, t, phase)
+
+            @pl.when(serves & (phase == 1) & (core == 0))
+            def _():
+                late_fold(t, 2 * tiles)
 
         for _, sign, s, t in near:
             side = inward * sign
             owner = me + side * s
             arrive(owner, hh, t, side, phase)
             if sign == -1 and s == 1:
-                @pl.when((phase == 0) & ~at_end)
+                if t == tiles - 1:
+                    @pl.when((phase == 0) & ~at_end)
+                    def _():
+                        for own_t in range(tiles):
+                            send(me, 1 - first, own_t, inward)
+            take(owner, hh, t, phase)
+            if sign == 1 and s == 1:
+                @pl.when(serves & (phase == 1) & (core == 0))
                 def _():
-                    send(me, 1 - first, t, inward)
-            take(owner, hh, t, phase)
+                    late_fold(tiles + t, 2 * tiles)
+
+                    if t == tiles - 1:
+                        finish_served()
 
         @pl.loop(3, n)
         def _(s):
@@ -233,33 +268,19 @@
                     arrive(me + side * s, hh, t, side, phase)
                     take(me + side * s, hh, t, phase)
 
-        @pl.when(serves & (hh == 0))
-        def _():
-            @pl.when(phase == 0)
-            def _():
-                for t in range(tiles):
-                    query_copy(t).wait_recv()
-
-                @pl.loop(0, n)
-                def _(owner):
-                    @pl.loop(0, tiles)
-                    def _(t):
-                        fold_into(2, end, owner, 0, t)
-
+        @pl.when(serves & (hh == 0) & (phase == 1))
+        def _():
             finish_served()
-            for h in range(heads):
-                out_ref[pl.ds(0, TILE), pl.ds(h * HD, HD)] = finish(0, 0, h)
-            done_copy(tiles - 1).start()
 
     for i in range(rows // TILE):
         for h in range(heads):
-            out_ref[pl.ds(i * TILE, TILE), pl.ds(q_half + h * HD, HD)] = finish(1, i, h)
+            keep(1, i, h)
 
     @pl.when(~at_end)
     def _():
         for i in range(rows // TILE):
             for h in range(heads):
-                out_ref[pl.ds(i * TILE, TILE), pl.ds(h * HD, HD)] = finish(0, i, h)
+                keep(0, i, h)
 
     count = jnp.sum((exits_vec[...] > 0).astype(jnp.int32))
     for d in range(1, n):
@@ -272,7 +293,7 @@
         for t in range(tiles):
             here = pl.ds(t * TILE, TILE)
             done_copy(t).wait_recv()
-            out_ref[here, pl.ds(0, q_half)] = done[1, here, :]
+            out_ref[here, pl.ds(0, q_half)] = live_only(t, done[1, here, :])
             query_copy(t).wait_send()
 
     @pl.when(serves)
@@ -310,17 +331,17 @@
             jax.ShapeDtypeStruct((rows, q_width), jnp.bfloat16),
             jax.ShapeDtypeStruct((1,), jnp.int32),
         ),
-        in_specs=[smem, vmem, hbm, hbm, hbm],
+        in_specs=[smem, smem, vmem, hbm, hbm, hbm],
         out_specs=(vmem, smem),
         scratch_shapes=[
-            pltpu.VMEM((3, rows, q_half), jnp.bfloat16),
+            pltpu.VMEM((3, q_half // HD, rows, HD), jnp.bfloat16),
             pltpu.VMEM((n, 2, tiles, 2, TILE, kv_half), jnp.bfloat16),
-            pltpu.VMEM((3, rows, q_half), jnp.float32),
-            pltpu.VMEM((3, q_half // HD, rows, TILE), jnp.float32),
+            pltpu.VMEM((3, rows * q_half // HD, HD), jnp.float32),
+            pltpu.VMEM((3, rows * q_half // HD, TILE), jnp.float32),
             pltpu.VMEM((2, rows, q_half), jnp.bfloat16),
             pltpu.VMEM((n - 1, 1, TILE), jnp.int32),
             dma((2, tiles, 2)),
-            dma((2,)),
+            dma((2, q_half // HD)),
             dma((2, n, 2, tiles)),
             dma((n, 2, tiles)),
             dma((tiles,)),
@@ -330,11 +351,11 @@
             dma((n - 1,)),
             dma((n - 1,)),
         ],
-        compiler_params=pltpu.CompilerParams(collective_id=0, has_side_effects=True),
+        compiler_params=pltpu.CompilerParams(
+            collective_id=0, has_side_effects=True, vmem_limit_bytes=64_000_000
+        ),
         name="attend_line",
-    )(tile_order, exits_vec, queries[0], keys[0], values[0])
-    live_rows = jnp.repeat(exit_layer > 0, TILE, total_repeat_length=rows)
-    attended = jnp.where(live_rows[:, None], attended, jnp.zeros((), jnp.bfloat16))
+    )(tile_order, exit_layer, exits_vec, queries[0], keys[0], values[0])
     return attended[None], live
 
 

time: 70 us -> 61.3 us (0.88)
  Pallas kernels: 61.4 us -> 55.4 us
  other arithmetic: 4.1 us -> 0 us
  local copies, waits for them, and re-layouts: 1.82 us -> 3.23 us
    pallas_call x1, Pallas kernels: 61.4 us -> 55.4 us  [body(): pl.pallas_call(functools.partial(kernel, n), out_shape=(jax.ShapeDtypeStr...]
    broadcast_in_dim x1 -> x0, other arithmetic: 2.14 us -> none  [body(): return (attended[None], live)]
    unnamed x2 -> x3, local copies, waits for them, and re-layouts: 0.65 us -> 2.71 us
    gather x1 -> x0, other arithmetic: 1.93 us -> none  [body(): live_rows = jnp.repeat(exit_layer > 0, TILE, total_repeat_length=rows)]
where the time goes in v3:
time: 61.3 us; the launch traced here: 61.1 us
  Pallas kernels  55.4 us (90%)
  local copies, waits for them, and re-layouts  3.23 us (5%)
  between operations  2.41 us (4%)
    pallas_call x1, Pallas kernels, body(): pl.pallas_call(functools.partial(kernel, n), out_shape=(jax.ShapeDtypeStr...  55.4 us
    unnamed x3, local copies, waits for them, and re-layouts  2.71 us

profile of v3, /device:TPU:0, one launch (start us, length us, event | category | flops | bytes accessed | tf_op | source)
XLA Modules:
  0.0 61.1 jit_solution(6247954407073155479)
XLA Ops:
  0.6 0.0 copy-start
  0.6 0.6 %copy-done = s32[3]{0:T(128)S(1)} copy-done((s32[3]{0:T(128)S(1)}, s32[3]{0:T(128)}, u32[]{:S(2)}) %copy-start) | copy-done | bytes 36
  1.3 0.5 pad_bitcast_fusion.exits_vec
  1.8 55.4 %attend_line.1 = (bf16[384,1024]{1,0:T(8,128)(2,1)}, s32[1]{0:T(128)}) custom-call(s32[12]{0:T(128)} %order_ref.1, s32[3]{0:T(128)} %exit_ref.1, s32[1,128]{1,0:T(1,128)} %pad_bitcast_fusion.exits_vec, bf16[384,1024]{1,0:T(8,128)(2,1)} %bitcast.6, bf16[384,512]{1,0:T(8,128)(2,1)} %bitcast.8, bf16[384,512]{1,0:T(8,128)(2,1)} %bitcast.9), custom_call_target="tpu_custom_call" | custom-call | tf_op jit(solution)/shard_map/attend_line/pallas_call | solution.py:328
  57.2 2.1 %copy.9 = bf16[1,384,1024]{2,1,0:T(8,128)(2,1)} copy(bf16[1,384,1024]{2,1,0:T(8,128)(2,1)} %bitcast.7) | data formatting | bytes 1572864
Async XLA Ops:
  0.6 0.7 %copy-start = (s32[3]{0:T(128)S(1)}, s32[3]{0:T(128)}, u32[]{:S(2)}) copy-start(s32[3]{0:T(128)} %exit_ref.1) | copy-start | bytes 40
